TPU v7x, 32 devices: a whole 2x2x4 slice. The times are simulated.
32 devices in a mesh: cell: 8 (over z, x), seq: 4 (over y, core).
Axes of the slice: x: 2, y: 2, z: 4, core: 2. Of those that a mesh axis runs over, the one named last changes fastest.
Arguments:
- cells_in: bfloat16 [8, 1024, 1120], P('cell', 'seq'), may hold values from -6 to 6
- dataset_ids: int32 [8], P('cell'), may hold values from 0 to 15
- cell_lengths: int32 [8], P('cell'), may hold values from 512 to 1024, as said below
- table: float32 [16, 1120], replicated, may hold values from -3 to 3
- wqkv: bfloat16 [1120, 3360], P('seq'), may hold values from -0.25 to 0.25
- bq: float32 [1120], replicated, may hold values from -3 to 3
- bv: float32 [1120], replicated, may hold values from -3 to 3
- wout: bfloat16 [1120, 1120], P('seq'), may hold values from -0.5 to 0.5
- bout: float32 [1120], replicated, may hold values from -2 to 2
- gain1: float32 [1120], replicated, may hold values from 0.1 to 1.9
- shift1: float32 [1120], replicated, may hold values from -2 to 2
- gain2: float32 [1120], replicated, may hold values from 0.1 to 1.9
- shift2: float32 [1120], replicated, may hold values from -2 to 2
- wup: bfloat16 [1120, 4480], P(None, 'cell'), may hold values from -0.1875 to 0.1875
- bup: float32 [4480], replicated, may hold values from -2 to 2
- wdown: bfloat16 [4480, 1120], P('cell'), may hold values from -0.09375 to 0.09375
- bdown: float32 [1120], replicated, may hold values from -2 to 2
- out_grad: bfloat16 [8, 1024, 1120], P('cell', 'seq'), may hold values from -6 to 6
Outputs:
- cells_out: bfloat16 [8, 1024, 1120], P('cell', 'seq')
- cells_grad: bfloat16 [8, 1024, 1120], P('cell', 'seq')
- grad_table: float32 [16, 1120], P(None, 'seq')
- grad_wqkv: float32 [1120, 3360], P('seq')
- grad_bq: float32 [1120], P('seq')
- grad_bv: float32 [1120], P('seq')
- grad_wout: float32 [1120, 1120], P('seq')
- grad_bout: float32 [1120], P('seq')
- grad_gain1: float32 [1120], P('seq')
- grad_shift1: float32 [1120], P('seq')
- grad_gain2: float32 [1120], P('seq')
- grad_shift2: float32 [1120], P('seq')
- grad_wup: float32 [1120, 4480], P(None, 'cell')
- grad_bup: float32 [4480], P('seq')
- grad_wdown: float32 [4480, 1120], P('cell')
- grad_bdown: float32 [1120], P('seq')
Inputs may be any that keep to these rules, and one draw needn't show every extreme that they name: `cell_lengths`: some cell has exactly 1024 live positions.
All inputs are finite; a program needn't handle non-finite values.
Results may differ from a plain program's by a relative error of at most 0.015.
Values may be sent and summed in bfloat16 or wider, within the bound.
A program may use at most 256 MiB of HBM per device.

v0:
```python
import math
import jax
import jax.numpy as jnp
from jax import lax
from jax.sharding import PartitionSpec as P

HEAD_DIM = 56
norm_eps = 1e-05


def cut_along(x, dim, size):
    lengths = x.shape
    parts = x.reshape(*lengths[:dim], size, lengths[dim] // size, *lengths[dim + 1 :])
    return jnp.moveaxis(parts, dim, 0)


def sent_and_summed(x, axis, dim):
    parts = cut_along(x, dim, lax.axis_size(axis))
    arrived = lax.all_to_all(parts, axis, split_axis=0, concat_axis=0, tiled=True)
    return arrived.astype(jnp.float32).sum(axis=0)


def product(left, right):
    return jnp.dot(left, right, preferred_element_type=jnp.float32)


def left_inner(left, right):
    return lax.dot_general(
        left, right, (((0,), (0,)), ((), ())), preferred_element_type=jnp.float32
    )


def right_inner(left, right):
    return lax.dot_general(
        left, right, (((1,), (1,)), ((), ())), preferred_element_type=jnp.float32
    )


def norm_forward(hidden, gain, shift):
    centre = hidden - jnp.mean(hidden, axis=-1, keepdims=True)
    inverse = lax.rsqrt(jnp.mean(centre * centre, axis=-1, keepdims=True) + norm_eps)
    unit_rows = centre * inverse
    return (unit_rows * gain + shift, unit_rows, inverse)


def norm_backward(grad_rows, unit_rows, inverse, gain):
    scaled = grad_rows * gain
    inside = (
        scaled
        - jnp.mean(scaled, axis=-1, keepdims=True)
        - unit_rows * jnp.mean(scaled * unit_rows, axis=-1, keepdims=True)
    )
    return (inside * inverse, jnp.sum(grad_rows * unit_rows, axis=0), jnp.sum(grad_rows, axis=0))


def block_scores(queries, keys_used, first_row, length, score_scale):
    row_count = queries.shape[0]
    key_count = keys_used.shape[0]
    scores = (
        jnp.einsum("qhd,khd->hqk", queries, keys_used, preferred_element_type=jnp.float32)
        * score_scale
    )
    query_pos = first_row + lax.broadcasted_iota(jnp.int32, (row_count, key_count), 0)
    key_pos = lax.broadcasted_iota(jnp.int32, (row_count, key_count), 1)
    visible = (key_pos <= query_pos) & (key_pos < length)
    return jnp.where(visible[None], scores, -1e30)


def attend_forward(query_heads, key_heads, value_heads, length, row_block, score_scale):
    slot_count = query_heads.shape[0]
    outputs = []
    logsums = []
    for block_idx in range(slot_count // row_block):
        first_row = block_idx * row_block
        key_count = first_row + row_block
        scores = block_scores(
            query_heads[first_row:key_count], key_heads[:key_count], first_row, length, score_scale
        )
        highest = jnp.max(scores, axis=-1, keepdims=True)
        weights = jnp.exp(scores - highest)
        denominator = jnp.sum(weights, axis=-1, keepdims=True)
        prob_low = (weights / denominator).astype(jnp.bfloat16)
        outputs.append(
            jnp.einsum(
                "hqk,khd->qhd",
                prob_low,
                value_heads[:key_count],
                preferred_element_type=jnp.float32,
            )
        )
        logsums.append(highest + jnp.log(denominator))
    return (jnp.concatenate(outputs, axis=0), logsums)


def attend_backward(
    query_heads, key_heads, value_heads, grad_heads, logsums, length, row_block, score_scale
):
    slot_count = query_heads.shape[0]
    grad_query = []
    grad_key = jnp.zeros(key_heads.shape, jnp.float32)
    grad_value = jnp.zeros(value_heads.shape, jnp.float32)
    for block_idx in range(slot_count // row_block):
        first_row = block_idx * row_block
        key_count = first_row + row_block
        queries = query_heads[first_row:key_count]
        grads_here = grad_heads[first_row:key_count]
        scores = block_scores(queries, key_heads[:key_count], first_row, length, score_scale)
        prob_full = jnp.exp(scores - logsums[block_idx])
        prob_low = prob_full.astype(jnp.bfloat16)
        grad_prob = jnp.einsum(
            "qhd,khd->hqk", grads_here, value_heads[:key_count], preferred_element_type=jnp.float32
        )
        grad_value = grad_value.at[:key_count].add(
            jnp.einsum("hqk,qhd->khd", prob_low, grads_here, preferred_element_type=jnp.float32)
        )
        row_inner = jnp.sum(prob_full * grad_prob, axis=-1, keepdims=True)
        grad_score = (prob_full * (grad_prob - row_inner)).astype(jnp.bfloat16)
        grad_query.append(
            jnp.einsum(
                "hqk,khd->qhd",
                grad_score,
                key_heads[:key_count],
                preferred_element_type=jnp.float32,
            )
            * score_scale
        )
        grad_key = grad_key.at[:key_count].add(
            jnp.einsum("hqk,qhd->khd", grad_score, queries, preferred_element_type=jnp.float32)
            * score_scale
        )
    return (jnp.concatenate(grad_query, axis=0), grad_key, grad_value)


def shards(
    cells_in,
    dataset_ids,
    cell_lengths,
    table,
    wqkv,
    bq,
    bv,
    wout,
    bout,
    gain1,
    shift1,
    gain2,
    shift2,
    wup,
    bup,
    wdown,
    bdown,
    out_grad,
):
    seq_count = lax.axis_size("seq")
    local_rows = cells_in.shape[1]
    width = cells_in.shape[2]
    slot_count = local_rows * seq_count
    group_width = width // seq_count
    heads_here = group_width // HEAD_DIM
    row_block = min(512, slot_count)
    score_scale = 1.0 / math.sqrt(HEAD_DIM)
    length = cell_lengths[0]
    dataset_pick = (
        lax.broadcasted_iota(jnp.int32, (1, table.shape[0]), 1) == dataset_ids[0]
    ).astype(jnp.float32)
    table_row = jnp.dot(
        dataset_pick, table, precision=lax.Precision.HIGHEST, preferred_element_type=jnp.float32
    )
    resid_in = cells_in[0].astype(jnp.float32) + table_row
    normed1, unit1, inverse1 = norm_forward(resid_in, gain1, shift1)
    normed1_low = normed1.astype(jnp.bfloat16)
    wqkv_full, wout_full = (
        lax.all_gather(wqkv, "seq", axis=0, tiled=True),
        lax.all_gather(wout, "seq", axis=0, tiled=True),
    )
    qkv_bias = jnp.concatenate([bq, jnp.zeros_like(bq), bv])
    qkv_low = (product(normed1_low, wqkv_full) + qkv_bias).astype(jnp.bfloat16)
    qkv_heads = lax.all_to_all(
        qkv_low.reshape(local_rows, 3, seq_count, group_width),
        "seq",
        split_axis=2,
        concat_axis=0,
        tiled=True,
    )
    query_heads = qkv_heads[:, 0, 0].reshape(slot_count, heads_here, HEAD_DIM)
    key_heads = qkv_heads[:, 1, 0].reshape(slot_count, heads_here, HEAD_DIM)
    value_heads = qkv_heads[:, 2, 0].reshape(slot_count, heads_here, HEAD_DIM)
    context, logsums = attend_forward(
        query_heads, key_heads, value_heads, length, row_block, score_scale
    )
    context_low = context.astype(jnp.bfloat16).reshape(slot_count, 1, group_width)
    context_rows = lax.all_to_all(
        context_low, "seq", split_axis=0, concat_axis=1, tiled=True
    ).reshape(local_rows, width)
    resid_mid = resid_in + product(context_rows, wout_full) + bout
    normed2, unit2, inverse2 = norm_forward(resid_mid, gain2, shift2)
    normed2_low = normed2.astype(jnp.bfloat16)
    wup_full, wdown_full = (
        lax.all_gather(wup, "cell", axis=1, tiled=True),
        lax.all_gather(wdown, "cell", axis=0, tiled=True),
    )
    up_rows = product(normed2_low, wup_full) + bup
    act_low = jax.nn.gelu(up_rows, approximate=True).astype(jnp.bfloat16)
    cells_out = (resid_mid + product(act_low, wdown_full) + bdown).astype(jnp.bfloat16)[None]
    grad_out = out_grad[0]
    grad_rows = grad_out.astype(jnp.float32)
    grad_bdown = jnp.sum(grad_rows, axis=0)
    grad_wdown = left_inner(act_low, grad_out)
    wup_back, wdown_back = (
        lax.all_gather(wup, "cell", axis=1, tiled=True),
        lax.all_gather(wdown, "cell", axis=0, tiled=True),
    )
    grad_act = right_inner(grad_out, wdown_back)
    gelu_pull = jax.vjp(lambda values: jax.nn.gelu(values, approximate=True), up_rows)[1]
    grad_up_low = gelu_pull(grad_act)[0].astype(jnp.bfloat16)
    grad_bup = jnp.sum(grad_up_low.astype(jnp.float32), axis=0)
    grad_wup = left_inner(normed2_low, grad_up_low)
    grad_norm2 = right_inner(grad_up_low, wup_back)
    back_second, grad_gain2, grad_shift2 = norm_backward(grad_norm2, unit2, inverse2, gain2)
    grad_mid = grad_rows + back_second
    grad_mid_low = grad_mid.astype(jnp.bfloat16)
    grad_bout = jnp.sum(grad_mid_low.astype(jnp.float32), axis=0)
    grad_context = right_inner(grad_mid_low, wout_full).astype(jnp.bfloat16)
    grad_context_heads = lax.all_to_all(
        grad_context.reshape(local_rows, seq_count, group_width),
        "seq",
        split_axis=1,
        concat_axis=0,
        tiled=True,
    ).reshape(slot_count, heads_here, HEAD_DIM)
    grad_query, grad_key, grad_value = attend_backward(
        query_heads,
        key_heads,
        value_heads,
        grad_context_heads,
        logsums,
        length,
        row_block,
        score_scale,
    )
    grad_qkv_heads = jnp.stack([grad_query, grad_key, grad_value], axis=1).astype(jnp.bfloat16)
    grad_qkv = lax.all_to_all(
        grad_qkv_heads.reshape(slot_count, 3, 1, group_width),
        "seq",
        split_axis=0,
        concat_axis=2,
        tiled=True,
    ).reshape(local_rows, 3 * width)
    grad_qkv_wide = grad_qkv.astype(jnp.float32)
    grad_bq = jnp.sum(grad_qkv_wide[:, :width], axis=0)
    grad_bv = jnp.sum(grad_qkv_wide[:, 2 * width :], axis=0)
    grad_norm1 = right_inner(grad_qkv, wqkv_full)
    back_first, grad_gain1, grad_shift1 = norm_backward(grad_norm1, unit1, inverse1, gain1)
    grad_in = grad_mid + back_first
    cells_grad = grad_in.astype(jnp.bfloat16)[None]
    grad_table = jnp.transpose(dataset_pick) * jnp.sum(grad_in, axis=0)[None, :]
    grad_wqkv = left_inner(normed1_low, grad_qkv)
    grad_wout = left_inner(context_rows, grad_mid_low)
    seq_parts = (
        lax.psum_scatter(
            grad_table.astype(jnp.bfloat16), "seq", scatter_dimension=1, tiled=True
        ).astype(jnp.float32),
        lax.psum_scatter(
            grad_wqkv.astype(jnp.bfloat16), "seq", scatter_dimension=0, tiled=True
        ).astype(jnp.float32),
        lax.psum_scatter(
            grad_wout.astype(jnp.bfloat16), "seq", scatter_dimension=0, tiled=True
        ).astype(jnp.float32),
        lax.psum_scatter(
            grad_bq.astype(jnp.bfloat16), "seq", scatter_dimension=0, tiled=True
        ).astype(jnp.float32),
        lax.psum_scatter(
            grad_bv.astype(jnp.bfloat16), "seq", scatter_dimension=0, tiled=True
        ).astype(jnp.float32),
        lax.psum_scatter(
            grad_bout.astype(jnp.bfloat16), "seq", scatter_dimension=0, tiled=True
        ).astype(jnp.float32),
        lax.psum_scatter(
            grad_gain1.astype(jnp.bfloat16), "seq", scatter_dimension=0, tiled=True
        ).astype(jnp.float32),
        lax.psum_scatter(
            grad_shift1.astype(jnp.bfloat16), "seq", scatter_dimension=0, tiled=True
        ).astype(jnp.float32),
        lax.psum_scatter(
            grad_gain2.astype(jnp.bfloat16), "seq", scatter_dimension=0, tiled=True
        ).astype(jnp.float32),
        lax.psum_scatter(
            grad_shift2.astype(jnp.bfloat16), "seq", scatter_dimension=0, tiled=True
        ).astype(jnp.float32),
        lax.psum_scatter(
            grad_bup.astype(jnp.bfloat16), "seq", scatter_dimension=0, tiled=True
        ).astype(jnp.float32),
        lax.psum_scatter(
            grad_bdown.astype(jnp.bfloat16), "seq", scatter_dimension=0, tiled=True
        ).astype(jnp.float32),
    )
    share_qkv = seq_parts[1]
    share_out = seq_parts[2]
    part_qkv, part_out = (
        sent_and_summed(share_qkv.reshape(-1).astype(jnp.bfloat16), "cell", 0),
        sent_and_summed(share_out.reshape(-1).astype(jnp.bfloat16), "cell", 0),
    )
    whole_qkv, whole_out = (
        lax.all_gather(part_qkv.astype(jnp.bfloat16), "cell", axis=0, tiled=True).astype(
            part_qkv.dtype
        ),
        lax.all_gather(part_out.astype(jnp.bfloat16), "cell", axis=0, tiled=True).astype(
            part_out.dtype
        ),
    )
    total_wqkv = whole_qkv.reshape(share_qkv.shape)
    total_wout = whole_out.reshape(share_out.shape)
    others = lax.psum((seq_parts[0],) + tuple(seq_parts[3:]), "cell")
    summed = (others[0], total_wqkv, total_wout) + tuple(others[1:])
    cell_up, cell_down = (
        lax.psum_scatter(grad_wup, "cell", scatter_dimension=1, tiled=True),
        lax.psum_scatter(grad_wdown, "cell", scatter_dimension=0, tiled=True),
    )
    total_up, total_down = (
        lax.psum(cell_up.astype(jnp.bfloat16), "seq").astype(jnp.float32),
        lax.psum(cell_down.astype(jnp.bfloat16), "seq").astype(jnp.float32),
    )
    return (
        cells_out,
        cells_grad,
        summed[0],
        summed[1],
        summed[3],
        summed[4],
        summed[2],
        summed[5],
        summed[6],
        summed[7],
        summed[8],
        summed[9],
        total_up,
        summed[10],
        total_down,
        summed[11],
    )


def solution(mesh):
    return jax.shard_map(
        shards,
        mesh=mesh,
        in_specs=(
            P("cell", "seq", None),
            P("cell"),
            P("cell"),
            P(),
            P("seq", None),
            P(),
            P(),
            P("seq", None),
            P(),
            P(),
            P(),
            P(),
            P(),
            P(None, "cell"),
            P(),
            P("cell", None),
            P(),
            P("cell", "seq", None),
        ),
        out_specs=(
            P("cell", "seq", None),
            P("cell", "seq", None),
            P(None, "seq"),
            P("seq", None),
            P("seq"),
            P("seq"),
            P("seq", None),
            P("seq"),
            P("seq"),
            P("seq"),
            P("seq"),
            P("seq"),
            P(None, "cell"),
            P("seq"),
            P("cell", None),
            P("seq"),
        ),
        check_vma=False,
    )
```

profile of v0, /device:TPU:0, one launch (start us, length us, event | category | flops | bytes accessed | tf_op | source)
XLA Modules:
  0.0 1535.5 jit_solution(6749002238563494380)
XLA Ops:
  11.5 55.4 %all-gather.5.cloned.1.call-done = bf16[1120,3360]{1,0:T(8,128)(2,1)} async-done(((bf16[280,3360]{1,0:T(8,128)(2,1)}), bf16[1120,3360]{1,0:T(8,128)(2,1)}) %all-gather.5.cloned.1.call-update) | async-done | bytes 7526416 | tf_op jit(solution)/shard_map/all_gather | solution.py:173
  67.0 7.2 fusion.6
  75.5 3.7 all-to-all-start
  81.1 29.6 %all-to-all-done = bf16[256,3,4,280]{0,3,1,2:T(8,128)(2,1)S(1)} async-done(((bf16[256,3,4,280]{0,3,1,2:T(8,128)(2,1)}), bf16[256,3,4,280]{0,3,1,2:T(8,128)(2,1)S(1)}, u32[]{:S(2)}, u32[]{:S(2)}) %all-to-all-start) | async-done | bytes 1720352 | tf_op jit(solution)/shard_map/all_to_all | solution.py:178
  113.8 2.2 fusion.101
  116.1 2.3 fusion
  120.0 3.1 fusion.44
  127.3 3.7 all-to-all-start.1
  131.0 9.3 all-to-all-done.1
  145.0 3.3 fusion.103
  148.6 106.2 %all-gather.9.cloned.1.call-done = bf16[1120,4480]{0,1:T(8,128)(2,1)} async-done(((bf16[1120,560]{0,1:T(8,128)(2,1)}), bf16[1120,4480]{0,1:T(8,128)(2,1)}) %all-gather.9.cloned.1.call-update) | async-done | bytes 10035216 | tf_op jit(solution)/shard_map/all_gather | solution.py:199
  254.8 9.8 convolution_add_fusion
  264.6 138.9 %all-gather.11.cloned.1.call-done = bf16[4480,1120]{1,0:T(8,128)(2,1)} async-done(((bf16[560,1120]{1,0:T(8,128)(2,1)}), bf16[4480,1120]{1,0:T(8,128)(2,1)}) %all-gather.11.cloned.1.call-update) | async-done | bytes 10035216 | tf_op jit(solution)/shard_map/all_gather | solution.py:200
  403.6 12.7 fusion.104
  416.3 10.1 multiply_reduce_fusion.2
  429.9 3.5 all-to-all-start.2
  433.4 2.4 convolution_convert_fusion.1
  435.9 6.7 all-to-all-done.2
  443.1 3.8 fusion.37
  446.9 6.0 multiply_reduce_fusion.1
  453.3 5.9 fusion.33
  459.2 3.1 copy.91
  462.3 5.6 multiply_convert_fusion.1
  469.6 5.7 multiply_reduce_fusion
  475.7 2.3 multiply_convert_fusion
  478.0 2.4 fusion.36
  480.5 4.6 copy.90
  486.6 4.2 fusion.46
  491.7 4.9 copy.89
  496.6 7.6 pad_maximum_fusion
  504.2 39.4 %all_to_all.75 = bf16[1024,3,1,280]{3,1,2,0:T(4,128)(2,1)S(1)} all-to-all(bf16[1024,3,1,280]{3,1,2,0:T(4,128)(2,1)S(1)} %pad_maximum_fusion), channel_id=1, replica_groups=mesh['cell'=8,'seq'=4] {'seq'}, dimensions={0} | all-to-all | bytes 3440640 | tf_op jit(solution)/shard_map/all_to_all | solution.py:242
  543.6 4.0 copy.100
  549.4 4.8 convolution_convert_fusion
  555.4 14.6 fusion.95
  570.1 13.7 fusion.73
  583.8 3.4 convert_element_type.246
  587.3 6.2 reduce.20
  593.5 2.5 reshape.518
  596.0 4.8 all-to-all-start.5
  600.9 20.7 %reduce-scatter.14.cloned.1.call-done = bf16[280,3360]{1,0:T(8,128)(2,1)} async-done(((bf16[1120,3360]{1,0:T(8,128)(2,1)}), bf16[280,3360]{1,0:T(8,128)(2,1)}) %reduce-scatter.14.cloned.1.call-update) | async-done | bytes 1881616
  621.6 5.4 reshape.512
  627.0 5.6 convert_element_type.245
  632.6 42.0 %reduce.19 = bf16[8,117600]{1,0:T(8,128)(2,1)} reduce(bf16[8,1,117600]{2,1,0:T(2,128)(2,1)} %convert_element_type.245, bf16[]{:T(256)} %broadcast.342), dimensions={1}, to_apply=%convert_element_type.245.reduce_sub_computation | reduce | bytes 3763202 | tf_op jit(solution)/shard_map/convert_element_type | solution.py:300
  674.5 4.7 reshape.516
  679.2 5.5 all-to-all-start.4
  690.1 4.1 reshape.519
  694.1 3.2 reduce_sum.247
  698.2 2.4 dynamic-update-slice.11
  700.5 73.5 %all-to-all-done.4 = bf16[8,2,58800]{2,1,0:T(2,128)(2,1)} async-done(((bf16[8,2,58800]{2,1,0:T(2,128)(2,1)}), bf16[8,2,58800]{2,1,0:T(2,128)(2,1)}, u32[]{:S(2)}, u32[]{:S(2)}) %all-to-all-start.4) | async-done | bytes 1881632 | tf_op jit(solution)/shard_map/all_to_all | solution.py:19
  774.0 7.9 reshape.517
  781.9 6.5 reduce_sum.244
  789.8 4.8 dynamic-update-slice.10
  794.8 11.3 fusion.23
  808.2 5.9 fusion.62
  815.6 188.3 %reduce-scatter.10.cloned.1.call-done = f32[1120,560]{0,1:T(8,128)} async-done(((f32[1120,4480]{0,1:T(8,128)}), f32[1120,560]{0,1:T(8,128)}) %reduce-scatter.10.cloned.1.call-update) | async-done | bytes 2508816 | tf_op jit(solution)/shard_map/reduce_scatter | solution.py:316
  1004.0 2.9 convert_element_type.238
  1006.9 336.9 %reduce-scatter.12.cloned.1.call-done = f32[560,1120]{1,0:T(8,128)} async-done(((f32[4480,1120]{1,0:T(8,128)}), f32[560,1120]{1,0:T(8,128)}) %reduce-scatter.12.cloned.1.call-update) | async-done | bytes 2508816 | tf_op jit(solution)/shard_map/reduce_scatter | solution.py:317
  1343.8 2.9 convert_element_type.241
  1347.4 12.6 all-reduce.18
  1360.8 38.1 %all-reduce.16 = (f32[16,280]{1,0:T(8,128)}, f32[280]{0:T(512)}, f32[280]{0:T(512)}, f32[280]{0:T(512)}, f32[280]{0:T(512)}, /*index=5*/f32[280]{0:T(512)}, f32[...) all-reduce(f32[16,280]{1,0:T(8,128)S(1)} %dynamic-slice_convert_fus, ...), channel_id=1, replica_groups=mesh['cell'=8,'seq'=4] {'cell'}, use_global_device_ids=true, to_apply=%region_16.17 | all-reduce | flops 7840 | bytes 62720 | tf_op jit(solution)/shard_map/psum | solution.py:313
  1399.0 63.3 %all-reduce.23.cloned.1.call-done = (bf16[940800]{0:T(1024)(128)(2,1)}, bf16[313600]{0:T(1024)(128)(2,1)}) async-done(((bf16[940800]{0:T(1024)(128)(2,1)}, bf16[313600]{0:T(1024)(128)(2,1)}), (bf16[940800]{0:T(1024)(128)(2,1)}, bf16[313600]{0:T(1024)(128)(2,1)})) %all-reduce.23.cloned.1.call-update) | async-done | bytes 2508816
  1462.3 5.5 reshape.482
  1469.6 54.1 %all-reduce.25.cloned.1.call-done = (bf16[1120,560]{0,1:T(8,128)(2,1)}, bf16[560,1120]{1,0:T(8,128)(2,1)}) async-done(((bf16[1120,560]{0,1:T(8,128)(2,1)}, bf16[560,1120]{1,0:T(8,128)(2,1)}), (bf16[1120,560]{0,1:T(8,128)(2,1)}, bf16[560,1120]{1,0:T(8,128)(2,1)})) %all-reduce.25.cloned.1.call-update) | async-done | bytes 2508816 | tf_op jit(solution)/shard_map/psum | solution.py:320
  1523.7 3.1 convert_element_type.239
  (205 shorter events, 45.5 us)
Async XLA Ops:
  7.2 3.6 copy-start
  7.2 3.5 copy-start.43
  7.2 3.5 copy-start.44
  7.2 3.8 copy-start.5
  7.2 59.7 %all-gather.5.cloned.1.call-start = ((), (), s32[]{:S(2)}) async-start(), calls=%async_computation.10 | async-start | bytes 9676800 | tf_op jit(solution)/shard_map/all_gather | solution.py:173
  8.0 59.0 %copy-start.35 = (f32[1120]{0:T(1024)S(1)}, f32[1120]{0:T(1024)}, u32[]{:S(2)}) copy-start(f32[1120]{0:T(1024)} %param.39) | copy-start | bytes 13444
  8.0 59.0 %copy-start.36 = (f32[1120]{0:T(1024)S(1)}, f32[1120]{0:T(1024)}, u32[]{:S(2)}) copy-start(f32[1120]{0:T(1024)} %param.40) | copy-start | bytes 13444
  8.0 137.0 %all-gather.7.cloned.1.call-start = ((), (), s32[]{:S(2)}) async-start(), calls=%async_computation.11 | async-start | bytes 3225600 | tf_op jit(solution)/shard_map/all_gather | solution.py:174
  8.7 246.1 %all-gather.9.cloned.1.call-start = ((), (), s32[]{:S(2)}) async-start(), calls=%async_computation.12 | async-start | bytes 11612160 | tf_op jit(solution)/shard_map/all_gather | solution.py:199
  9.5 394.1 %all-gather.11.cloned.1.call-start = ((), (), s32[]{:S(2)}) async-start(), calls=%async_computation.13 | async-start | bytes 11612160 | tf_op jit(solution)/shard_map/all_gather | solution.py:200
  11.5 62.7 %copy-start.39 = (f32[256]{0:T(256)}, f32[256]{0:T(256)S(1)}, u32[]{:S(2)}) copy-start(f32[256]{0:T(256)S(1)} %add_rsqrt_fusion.1) | copy-start | bytes 3076
  75.5 35.3 %all-to-all-start = ((bf16[256,3,4,280]{0,3,1,2:T(8,128)(2,1)}), bf16[256,3,4,280]{0,3,1,2:T(8,128)(2,1)S(1)}, u32[]{:S(2)}, u32[]{:S(2)}) async-start(bf16[256,3,4,280]{0,3,1,2:T(8,128)(2,1)} %copy.78), calls=%async_computation | async-start | bytes 3440640 | tf_op jit(solution)/shard_map/all_to_all | solution.py:178
  111.1 2.0 copy-start.19
  111.1 2.0 copy-start.20
  111.1 2.7 copy-start.15
  111.1 7.3 copy-start.29
  111.2 8.2 copy-start.23
  113.1 5.3 copy-start.3
  116.1 3.9 copy-start.2
  127.3 13.0 all-to-all-start.1
  142.4 2.6 copy-start.49
  145.0 3.4 copy-start.26
  145.0 109.8 %copy-start.33 = (f32[1120]{0:T(1024)S(1)}, f32[1120]{0:T(1024)}, u32[]{:S(2)}) copy-start(f32[1120]{0:T(1024)} %param.41) | copy-start | bytes 13444
  145.0 109.8 %copy-start.34 = (f32[1120]{0:T(1024)S(1)}, f32[1120]{0:T(1024)}, u32[]{:S(2)}) copy-start(f32[1120]{0:T(1024)} %param.42) | copy-start | bytes 13444
  145.0 109.8 %copy-start.48 = (f32[4480]{0:T(1024)S(1)}, f32[4480]{0:T(1024)}, u32[]{:S(2)}) copy-start(f32[4480]{0:T(1024)} %param.44) | copy-start | bytes 53764
  148.4 278.0 %copy-start.7 = (f32[256,1120]{0,1:T(8,128)}, f32[256,1120]{0,1:T(8,128)S(1)}, u32[]{:S(2)}) copy-start(f32[256,1120]{0,1:T(8,128)S(1)} %get-tuple-element.131) | copy-start | bytes 3440644
  148.6 277.8 %copy-start.37 = (f32[256]{0:T(256)}, f32[256]{0:T(256)S(1)}, u32[]{:S(2)}) copy-start(f32[256]{0:T(256)S(1)} %add_rsqrt_fusion) | copy-start | bytes 3076
  148.6 255.0 %copy-start.14 = (bf16[1,256,1120]{1,2,0:T(8,128)(2,1)S(1)}, bf16[1,256,1120]{1,2,0:T(8,128)(2,1)}, u32[]{:S(2)}) copy-start(bf16[1,256,1120]{1,2,0:T(8,128)(2,1)} %param.47) | copy-start | bytes 1720324
  416.3 10.1 copy-start.22
  426.4 1.7 copy-start.47
  427.6 5.8 copy-start.9
  428.1 5.3 copy-start.27
  429.9 12.8 all-to-all-start.2
  433.3 150.5 %reduce-scatter.16.cloned.1.call-start = ((), (), s32[]{:S(2)}) async-start(), calls=%async_computation.17 | async-start | bytes 3225600
  435.9 185.7 %reduce-scatter.14.cloned.1.call-start = ((), (), s32[]{:S(2)}) async-start(), calls=%async_computation.16 | async-start | bytes 9676800
  443.1 3.8 copy-start.30
  453.3 5.9 copy-start.17
  462.3 5.6 copy-start.21
  462.3 7.3 copy-start.18
  462.3 7.3 copy-start.24
  467.9 7.5 slice-start
  469.6 5.8 slice-start.1
  469.6 6.0 slice-start.2
  475.7 2.3 copy-start.16
  475.7 2.3 copy-start.25
  478.0 2.5 copy-start.4
  490.8 5.8 copy-start.12
  490.8 5.8 copy-start.13
  547.6 1.8 copy-start.6
  547.6 1.8 copy-start.40
  554.2 449.7 %reduce-scatter.10.cloned.1.call-start = ((), (), s32[]{:S(2)}) async-start(), calls=%async_computation.14 | async-start | bytes 23224320 | tf_op jit(solution)/shard_map/reduce_scatter | solution.py:316
  570.0 773.7 %reduce-scatter.12.cloned.1.call-start = ((), (), s32[]{:S(2)}) async-start(), calls=%async_computation.15 | async-start | bytes 23224320 | tf_op jit(solution)/shard_map/reduce_scatter | solution.py:317
  596.0 83.2 %all-to-all-start.5 = ((bf16[8,2,19600]{2,1,0:T(2,128)(2,1)}), bf16[8,2,19600]{2,1,0:T(2,128)(2,1)}, u32[]{:S(2)}, u32[]{:S(2)}) async-start(bf16[8,2,19600]{2,1,0:T(2,128)(2,1)} %reshape.518), calls=%async_computation.5 | async-start | bytes 1261568 | tf_op jit(solution)/shard_map/all_to_all | solution.py:19
  679.2 7.1 copy-start.52
  679.2 9.0 copy-start.51
  679.2 94.8 %all-to-all-start.4 = ((bf16[8,2,58800]{2,1,0:T(2,128)(2,1)}), bf16[8,2,58800]{2,1,0:T(2,128)(2,1)}, u32[]{:S(2)}, u32[]{:S(2)}) async-start(bf16[8,2,58800]{2,1,0:T(2,128)(2,1)} %reshape.516), calls=%async_computation.4 | async-start | bytes 3768320 | tf_op jit(solution)/shard_map/all_to_all | solution.py:19
  684.7 777.5 %all-reduce.23.cloned.1.call-start = ((), (), s32[]{:S(2)}) async-start(), calls=%async_computation.18 | async-start | bytes 5021696
  788.4 6.4 copy-start.50
  794.6 729.1 %all-reduce.25.cloned.1.call-start = ((), (), s32[]{:S(2)}) async-start(), calls=%async_computation.19 | async-start | bytes 5160960 | tf_op jit(solution)/shard_map/psum | solution.py:320
  808.2 5.9 copy-start.10
  1006.9 339.9 %copy-start.11 = (f32[256,3360]{0,1:T(8,128)S(1)}, f32[256,3360]{0,1:T(8,128)}, u32[]{:S(2)}) copy-start(f32[256,3360]{0,1:T(8,128)} %convert_element_type.222) | copy-start | bytes 10321924
  1462.3 5.5 copy-start.32
  1523.7 3.1 copy-start.28
  1523.7 4.7 copy-start.1
  (7 other events, 6.3 us)
Sparse Core Ops, SparseCore 0:
  9.6 57.3 all-gather.4
  68.5 35.2 all-gather.6
  106.0 148.7 all-gather.8
  256.9 146.6 all-gather.10
  437.0 33.1 reduce-scatter.15
  554.3 67.1 reduce-scatter.13
  625.5 378.4 reduce-scatter.9
  1007.9 335.8 reduce-scatter.11
  1348.6 113.6 all-reduce.22
  1465.2 58.4 all-reduce.24
where the time goes:
time: 1540 us
  waiting for transfers between devices  1090 us (71%)
  matrix products  136 us (9%)
  other arithmetic  98.1 us (6%)
  blocking collectives  90.2 us (6%)
  local copies, waits for them, and re-layouts  83.7 us (5%)
  starting transfers between devices  22.3 us (1%)
  between operations  19.2 us (1%)
    reduce_scatter x1, waiting for transfers between devices, shards(): lax.psum_scatter(grad_wdown, 'cell', scatter_dimension=0, tiled=True)  337 us
    reduce_scatter x1, waiting for transfers between devices, shards(): lax.psum_scatter(grad_wup, 'cell', scatter_dimension=1, tiled=True)  188 us
    all_gather x1, waiting for transfers between devices, shards(): lax.all_gather(wdown, 'cell', axis=0, tiled=True)  139 us
    all_gather x1, waiting for transfers between devices, shards(): lax.all_gather(wup, 'cell', axis=1, tiled=True)  106 us
    unnamed x13, waiting for transfers between devices  86.7 us
    all_to_all x2, waiting for transfers between devices, sent_and_summed(): lax.all_to_all(parts, axis, split_axis=0, concat_axis=0, tiled=True)  73.5 us
    all_gather x1, waiting for transfers between devices, shards(): lax.all_gather(wqkv, 'seq', axis=0, tiled=True)  55.4 us
    psum x1, waiting for transfers between devices, shards(): lax.psum(cell_up.astype(jnp.bfloat16), 'seq').astype(jnp.float32)  54.1 us
  transfers between devices with their start and end apart: 15, of which 12 were waited for; matrix products, arithmetic and copies ran while one was open for 18% of the time, Pallas kernels for 0%

commit v1 on v0

--- a/solution.py
+++ b/solution.py
@@ -6,6 +6,29 @@
 
 HEAD_DIM = 56
 norm_eps = 1e-05
+
+
+def cut_along_2(value, dim, count):
+    dims = value.shape
+    pieces = value.reshape(*dims[:dim], count, dims[dim] // count, *dims[dim + 1 :])
+    return jnp.moveaxis(pieces, dim, 0)
+
+
+def laid_out(pieces, dim):
+    pieces = jnp.moveaxis(pieces, 0, dim)
+    lengths = pieces.shape
+    return pieces.reshape(*lengths[:dim], lengths[dim] * lengths[dim + 1], *lengths[dim + 2 :])
+
+
+def pairwise_exchange(x, axis, split_dim, concat_dim):
+    size, index = (lax.axis_size(axis), lax.axis_index(axis))
+    blocks = cut_along_2(x, split_dim, size)
+    finished = [blocks[index]]
+    for turn in range(1, size):
+        sent = blocks[index ^ turn]
+        finished.append(lax.ppermute(sent, axis, [(i, i ^ turn) for i in range(size)]))
+    blocks = jnp.stack(finished)[index ^ jnp.arange(size)]
+    return laid_out(blocks, concat_dim)
 
 
 def cut_along(x, dim, size):
@@ -239,12 +262,8 @@
         score_scale,
     )
     grad_qkv_heads = jnp.stack([grad_query, grad_key, grad_value], axis=1).astype(jnp.bfloat16)
-    grad_qkv = lax.all_to_all(
-        grad_qkv_heads.reshape(slot_count, 3, 1, group_width),
-        "seq",
-        split_axis=0,
-        concat_axis=2,
-        tiled=True,
+    grad_qkv = pairwise_exchange(
+        grad_qkv_heads.reshape(slot_count, 3, 1, group_width), "seq", 0, 2
     ).reshape(local_rows, 3 * width)
     grad_qkv_wide = grad_qkv.astype(jnp.float32)
     grad_bq = jnp.sum(grad_qkv_wide[:, :width], axis=0)

time: 1540 us -> 1500 us (0.974)
  blocking collectives: 90.2 us -> 50.7 us
  waiting for transfers between devices: 1090 us -> 1110 us
    all_to_all x1 -> x0, blocking collectives: 39.4 us -> none  [shards(): lax.all_to_all(grad_qkv_heads.reshape(slot_count, 3, 1, group_width), 'se...]
    ppermute x0 -> x3, waiting for transfers between devices: none -> 19.1 us  [pairwise_exchange(): lax.ppermute(sent, axis, [(i, i ^ turn) for i in range(size)])]
    unnamed x126 -> x134, local copies, waits for them, and re-layouts: 43.3 us -> 46.1 us
  transfers between devices with their start and end apart: 15 -> 18, of which waited for: 12 -> 14; matrix products, arithmetic and copies ran while one was open for 18% -> 17% of each run, Pallas kernels for 0% -> 0%
where the time goes in v1:
time: 1500 us; the launch traced here: 1490 us
  waiting for transfers between devices  1110 us (74%)
  matrix products  128 us (9%)
  other arithmetic  87.2 us (6%)
  local copies, waits for them, and re-layouts  73.2 us (5%)
  blocking collectives  50.7 us (3%)
  starting transfers between devices  24.6 us (2%)
  between operations  19.3 us (1%)
    reduce_scatter x1, waiting for transfers between devices, shards(): lax.psum_scatter(grad_wdown, 'cell', scatter_dimension=0, tiled=True)  337 us
    reduce_scatter x1, waiting for transfers between devices, shards(): lax.psum_scatter(grad_wup, 'cell', scatter_dimension=1, tiled=True)  189 us
    all_gather x1, waiting for transfers between devices, shards(): lax.all_gather(wdown, 'cell', axis=0, tiled=True)  139 us
    all_gather x1, waiting for transfers between devices, shards(): lax.all_gather(wup, 'cell', axis=1, tiled=True)  106 us
    unnamed x13, waiting for transfers between devices  86.5 us
    all_to_all x2, waiting for transfers between devices, sent_and_summed(): lax.all_to_all(parts, axis, split_axis=0, concat_axis=0, tiled=True)  75 us
    all_gather x1, waiting for transfers between devices, shards(): lax.all_gather(wqkv, 'seq', axis=0, tiled=True)  55.4 us
    psum x1, waiting for transfers between devices, shards(): lax.psum(cell_up.astype(jnp.bfloat16), 'seq').astype(jnp.float32)  54.1 us
  transfers between devices with their start and end apart: 18, of which 14 were waited for; matrix products, arithmetic and copies ran while one was open for 17% of the time, Pallas kernels for 0%

profile of v1, /device:TPU:0, one launch (start us, length us, event | category | flops | bytes accessed | tf_op | source)
XLA Modules:
  0.0 1489.7 jit_solution(8222291721497306275)
XLA Ops:
  11.5 55.4 %all-gather.5.cloned.1.call-done = bf16[1120,3360]{1,0:T(8,128)(2,1)} async-done(((bf16[280,3360]{1,0:T(8,128)(2,1)}), bf16[1120,3360]{1,0:T(8,128)(2,1)}) %all-gather.5.cloned.1.call-update) | async-done | bytes 7526416 | tf_op jit(solution)/shard_map/all_gather | solution.py:196
  67.0 7.2 fusion.6
  75.5 4.2 all-to-all-start
  81.6 29.2 %all-to-all-done = bf16[256,3,4,280]{0,3,1,2:T(8,128)(2,1)S(1)} async-done(((bf16[256,3,4,280]{0,3,1,2:T(8,128)(2,1)}), bf16[256,3,4,280]{0,3,1,2:T(8,128)(2,1)S(1)}, u32[]{:S(2)}, u32[]{:S(2)}) %all-to-all-start) | async-done | bytes 1720352 | tf_op jit(solution)/shard_map/all_to_all | solution.py:201
  113.8 2.2 fusion.102
  116.1 2.3 fusion
  120.0 3.1 fusion.44
  125.2 2.2 reshape.534
  127.3 3.6 all-to-all-start.1
  131.0 9.3 all-to-all-done.1
  140.3 2.0 reshape.535
  142.3 2.1 copy.94
  145.0 3.3 fusion.104
  148.6 105.9 %all-gather.9.cloned.1.call-done = bf16[1120,4480]{0,1:T(8,128)(2,1)} async-done(((bf16[1120,560]{0,1:T(8,128)(2,1)}), bf16[1120,4480]{0,1:T(8,128)(2,1)}) %all-gather.9.cloned.1.call-update) | async-done | bytes 10035216 | tf_op jit(solution)/shard_map/all_gather | solution.py:222
  254.4 9.8 convolution_add_fusion
  264.2 138.9 %all-gather.11.cloned.1.call-done = bf16[4480,1120]{1,0:T(8,128)(2,1)} async-done(((bf16[560,1120]{1,0:T(8,128)(2,1)}), bf16[4480,1120]{1,0:T(8,128)(2,1)}) %all-gather.11.cloned.1.call-update) | async-done | bytes 10035216 | tf_op jit(solution)/shard_map/all_gather | solution.py:223
  403.2 12.5 fusion.105
  415.7 10.1 multiply_reduce_fusion.2
  429.3 3.5 all-to-all-start.2
  432.8 2.4 convolution_convert_fusion.1
  435.3 6.7 all-to-all-done.2
  443.7 4.0 multiply_reduce_fusion.1
  447.7 4.3 multiply_convert_fusion.1
  453.3 3.6 multiply_reduce_fusion
  456.9 2.3 multiply_convert_fusion
  462.4 2.5 stack.24
  465.8 3.5 fusion.36
  469.8 3.5 fusion.37
  473.3 5.8 fusion.33
  481.9 10.3 collective-permute-done.2
  492.2 8.8 collective-permute-done.1
  503.0 4.8 convolution_convert_fusion
  509.0 14.6 fusion.96
  524.7 13.4 fusion.73
  538.1 3.4 convert_element_type.246
  541.6 6.2 reduce.20
  547.8 2.5 reshape.538
  550.3 4.8 all-to-all-start.4
  555.1 20.4 %reduce-scatter.14.cloned.1.call-done = bf16[280,3360]{1,0:T(8,128)(2,1)} async-done(((bf16[1120,3360]{1,0:T(8,128)(2,1)}), bf16[280,3360]{1,0:T(8,128)(2,1)}) %reduce-scatter.14.cloned.1.call-update) | async-done | bytes 1881616
  575.6 5.4 reshape.532
  581.0 5.6 convert_element_type.245
  586.6 42.0 %reduce.19 = bf16[8,117600]{1,0:T(8,128)(2,1)} reduce(bf16[8,1,117600]{2,1,0:T(2,128)(2,1)} %convert_element_type.245, bf16[]{:T(256)} %broadcast.377), dimensions={1}, to_apply=%convert_element_type.245.reduce_sub_computation | reduce | bytes 3763202 | tf_op jit(solution)/shard_map/convert_element_type | solution.py:319
  628.5 4.7 reshape.536
  633.2 5.5 all-to-all-start.3
  643.2 4.1 reshape.539
  647.3 2.5 reduce_sum.247
  650.7 2.3 dynamic-update-slice.11
  653.0 75.0 %all-to-all-done.3 = bf16[8,2,58800]{2,1,0:T(2,128)(2,1)} async-done(((bf16[8,2,58800]{2,1,0:T(2,128)(2,1)}), bf16[8,2,58800]{2,1,0:T(2,128)(2,1)}, u32[]{:S(2)}, u32[]{:S(2)}) %all-to-all-start.3) | async-done | bytes 1881632 | tf_op jit(solution)/shard_map/all_to_all | solution.py:42
  728.0 7.9 reshape.537
  735.9 5.8 reduce_sum.244
  743.1 4.7 dynamic-update-slice.10
  748.0 11.3 fusion.23
  759.3 2.0 convert_element_type.222
  761.4 5.9 fusion.62
  768.7 189.3 %reduce-scatter.10.cloned.1.call-done = f32[1120,560]{0,1:T(8,128)} async-done(((f32[1120,4480]{0,1:T(8,128)}), f32[1120,560]{0,1:T(8,128)}) %reduce-scatter.10.cloned.1.call-update) | async-done | bytes 2508816 | tf_op jit(solution)/shard_map/reduce_scatter | solution.py:335
  958.0 2.9 convert_element_type.238
  960.9 337.0 %reduce-scatter.12.cloned.1.call-done = f32[560,1120]{1,0:T(8,128)} async-done(((f32[4480,1120]{1,0:T(8,128)}), f32[560,1120]{1,0:T(8,128)}) %reduce-scatter.12.cloned.1.call-update) | async-done | bytes 2508816 | tf_op jit(solution)/shard_map/reduce_scatter | solution.py:336
  1297.9 2.9 convert_element_type.241
  1301.6 12.6 all-reduce.18
  1315.0 38.1 %all-reduce.16 = (f32[16,280]{1,0:T(8,128)}, f32[280]{0:T(512)}, f32[280]{0:T(512)}, f32[280]{0:T(512)}, f32[280]{0:T(512)}, /*index=5*/f32[280]{0:T(512)}, f32[...) all-reduce(f32[16,280]{1,0:T(8,128)S(1)} %dynamic-slice_convert_fus, ...), channel_id=1, replica_groups=mesh['cell'=8,'seq'=4] {'cell'}, use_global_device_ids=true, to_apply=%region_16.17 | all-reduce | flops 7840 | bytes 62720 | tf_op jit(solution)/shard_map/psum | solution.py:332
  1353.1 63.4 %all-reduce.23.cloned.1.call-done = (bf16[940800]{0:T(1024)(128)(2,1)}, bf16[313600]{0:T(1024)(128)(2,1)}) async-done(((bf16[940800]{0:T(1024)(128)(2,1)}, bf16[313600]{0:T(1024)(128)(2,1)}), (bf16[940800]{0:T(1024)(128)(2,1)}, bf16[313600]{0:T(1024)(128)(2,1)})) %all-reduce.23.cloned.1.call-update) | async-done | bytes 2508816
  1416.5 5.5 reshape.492
  1423.8 54.1 %all-reduce.25.cloned.1.call-done = (bf16[1120,560]{0,1:T(8,128)(2,1)}, bf16[560,1120]{1,0:T(8,128)(2,1)}) async-done(((bf16[1120,560]{0,1:T(8,128)(2,1)}, bf16[560,1120]{1,0:T(8,128)(2,1)}), (bf16[1120,560]{0,1:T(8,128)(2,1)}, bf16[560,1120]{1,0:T(8,128)(2,1)})) %all-reduce.25.cloned.1.call-update) | async-done | bytes 2508816 | tf_op jit(solution)/shard_map/psum | solution.py:339
  1477.9 3.1 convert_element_type.239
  (222 shorter events, 42.1 us)
Async XLA Ops:
  7.2 3.6 copy-start
  7.2 3.5 copy-start.46
  7.2 3.5 copy-start.47
  7.2 3.8 copy-start.5
  7.2 59.7 %all-gather.5.cloned.1.call-start = ((), (), s32[]{:S(2)}) async-start(), calls=%async_computation.9 | async-start | bytes 9676800 | tf_op jit(solution)/shard_map/all_gather | solution.py:196
  8.0 59.0 %copy-start.38 = (f32[1120]{0:T(1024)S(1)}, f32[1120]{0:T(1024)}, u32[]{:S(2)}) copy-start(f32[1120]{0:T(1024)} %param.39) | copy-start | bytes 13444
  8.0 59.0 %copy-start.39 = (f32[1120]{0:T(1024)S(1)}, f32[1120]{0:T(1024)}, u32[]{:S(2)}) copy-start(f32[1120]{0:T(1024)} %param.40) | copy-start | bytes 13444
  8.0 137.0 %all-gather.7.cloned.1.call-start = ((), (), s32[]{:S(2)}) async-start(), calls=%async_computation.10 | async-start | bytes 3225600 | tf_op jit(solution)/shard_map/all_gather | solution.py:197
  8.7 245.7 %all-gather.9.cloned.1.call-start = ((), (), s32[]{:S(2)}) async-start(), calls=%async_computation.11 | async-start | bytes 11612160 | tf_op jit(solution)/shard_map/all_gather | solution.py:222
  9.5 393.7 %all-gather.11.cloned.1.call-start = ((), (), s32[]{:S(2)}) async-start(), calls=%async_computation.12 | async-start | bytes 11612160 | tf_op jit(solution)/shard_map/all_gather | solution.py:223
  11.5 62.7 %copy-start.42 = (f32[256]{0:T(256)}, f32[256]{0:T(256)S(1)}, u32[]{:S(2)}) copy-start(f32[256]{0:T(256)S(1)} %add_rsqrt_fusion.1) | copy-start | bytes 3076
  75.5 35.3 %all-to-all-start = ((bf16[256,3,4,280]{0,3,1,2:T(8,128)(2,1)}), bf16[256,3,4,280]{0,3,1,2:T(8,128)(2,1)S(1)}, u32[]{:S(2)}, u32[]{:S(2)}) async-start(bf16[256,3,4,280]{0,3,1,2:T(8,128)(2,1)} %copy.90), calls=%async_computation | async-start | bytes 3440640 | tf_op jit(solution)/shard_map/all_to_all | solution.py:201
  111.1 2.0 copy-start.19
  111.1 2.0 copy-start.21
  111.1 2.7 copy-start.15
  111.1 7.3 copy-start.32
  111.2 8.2 copy-start.26
  113.1 5.3 copy-start.3
  116.1 3.9 copy-start.2
  127.3 12.9 all-to-all-start.1
  142.3 2.6 copy-start.52
  144.9 3.4 copy-start.29
  145.0 109.5 %copy-start.36 = (f32[1120]{0:T(1024)S(1)}, f32[1120]{0:T(1024)}, u32[]{:S(2)}) copy-start(f32[1120]{0:T(1024)} %param.41) | copy-start | bytes 13444
  145.0 109.4 %copy-start.37 = (f32[1120]{0:T(1024)S(1)}, f32[1120]{0:T(1024)}, u32[]{:S(2)}) copy-start(f32[1120]{0:T(1024)} %param.42) | copy-start | bytes 13444
  145.0 109.4 %copy-start.51 = (f32[4480]{0:T(1024)S(1)}, f32[4480]{0:T(1024)}, u32[]{:S(2)}) copy-start(f32[4480]{0:T(1024)} %param.44) | copy-start | bytes 53764
  148.3 277.5 %copy-start.8 = (f32[256,1120]{0,1:T(8,128)}, f32[256,1120]{0,1:T(8,128)S(1)}, u32[]{:S(2)}) copy-start(f32[256,1120]{0,1:T(8,128)S(1)} %get-tuple-element.135) | copy-start | bytes 3440644
  148.5 277.3 %copy-start.40 = (f32[256]{0:T(256)}, f32[256]{0:T(256)S(1)}, u32[]{:S(2)}) copy-start(f32[256]{0:T(256)S(1)} %add_rsqrt_fusion) | copy-start | bytes 3076
  148.5 254.6 %copy-start.13 = (bf16[1,256,1120]{1,2,0:T(8,128)(2,1)S(1)}, bf16[1,256,1120]{1,2,0:T(8,128)(2,1)}, u32[]{:S(2)}) copy-start(bf16[1,256,1120]{1,2,0:T(8,128)(2,1)} %param.47) | copy-start | bytes 1720324
  415.7 10.1 copy-start.25
  427.0 5.8 copy-start.10
  427.5 5.3 copy-start.30
  429.3 12.8 all-to-all-start.2
  432.7 105.4 %reduce-scatter.16.cloned.1.call-start = ((), (), s32[]{:S(2)}) async-start(), calls=%async_computation.16 | async-start | bytes 3225600
  435.3 8.3 copy-start.33
  435.3 140.3 %reduce-scatter.14.cloned.1.call-start = ((), (), s32[]{:S(2)}) async-start(), calls=%async_computation.15 | async-start | bytes 9676800
  443.6 4.0 copy-start.23
  443.7 8.9 slice-start
  443.7 8.9 slice-start.1
  447.7 4.3 copy-start.20
  447.7 4.9 slice-start.2
  459.2 2.3 copy-start.4
  461.5 3.3 copy-start.22
  462.4 3.4 copy-start.16
  465.8 4.0 copy-start.24
  469.8 3.5 copy-start.18
  473.3 6.3 copy-start.28
  479.9 12.3 collective-permute-start.2
  480.2 20.8 %collective-permute-start.1 = (bf16[256,3,1,280]{0,3,2,1:T(8,128)(2,1)S(1)}, bf16[256,3,1,280]{0,3,2,1:T(8,128)(2,1)S(1)}, u32[]{:S(2)}, u32[]{:S(2)}) collective-permute-start(bf16[256,3,1,280]{0,3,2,1:T(8,128)(2,1)S(1)} %get-tuple-element.120), channel_id=1, source_target_pairs={{0,2},{1,3},{2,0},{3,1},{4,6},{5,7},{6,4},{7,5},{8,10},{9,11},{10,... | collective-permute-start | bytes 1290248 | tf_op jit(solution)/shard_map/ppermute | solution.py:29
  481.3 19.8 %collective-permute-start = (bf16[256,3,1,280]{0,3,2,1:T(8,128)(2,1)S(1)}, bf16[256,3,1,280]{0,3,2,1:T(8,128)(2,1)S(1)}, u32[]{:S(2)}, u32[]{:S(2)}) collective-permute-start(bf16[256,3,1,280]{0,3,2,1:T(8,128)(2,1)S(1)} %get-tuple-element.121), channel_id=1, source_target_pairs={{0,1},{1,0},{2,3},{3,2},{4,5},{5,4},{6,7},{7,6},{8,9},{9,8},{10,11... | collective-permute-start | bytes 1290248 | tf_op jit(solution)/shard_map/ppermute | solution.py:29
  507.8 450.2 %reduce-scatter.10.cloned.1.call-start = ((), (), s32[]{:S(2)}) async-start(), calls=%async_computation.13 | async-start | bytes 23224320 | tf_op jit(solution)/shard_map/reduce_scatter | solution.py:335
  523.6 774.3 %reduce-scatter.12.cloned.1.call-start = ((), (), s32[]{:S(2)}) async-start(), calls=%async_computation.14 | async-start | bytes 23224320 | tf_op jit(solution)/shard_map/reduce_scatter | solution.py:336
  550.3 82.9 %all-to-all-start.4 = ((bf16[8,2,19600]{2,1,0:T(2,128)(2,1)}), bf16[8,2,19600]{2,1,0:T(2,128)(2,1)}, u32[]{:S(2)}, u32[]{:S(2)}) async-start(bf16[8,2,19600]{2,1,0:T(2,128)(2,1)} %reshape.538), calls=%async_computation.4 | async-start | bytes 1261568 | tf_op jit(solution)/shard_map/all_to_all | solution.py:42
  633.2 6.2 copy-start.55
  633.2 8.1 copy-start.54
  633.2 94.8 %all-to-all-start.3 = ((bf16[8,2,58800]{2,1,0:T(2,128)(2,1)}), bf16[8,2,58800]{2,1,0:T(2,128)(2,1)}, u32[]{:S(2)}, u32[]{:S(2)}) async-start(bf16[8,2,58800]{2,1,0:T(2,128)(2,1)} %reshape.536), calls=%async_computation.3 | async-start | bytes 3768320 | tf_op jit(solution)/shard_map/all_to_all | solution.py:42
  638.7 777.8 %all-reduce.23.cloned.1.call-start = ((), (), s32[]{:S(2)}) async-start(), calls=%async_computation.17 | async-start | bytes 5021696
  741.7 6.3 copy-start.53
  747.8 730.1 %all-reduce.25.cloned.1.call-start = ((), (), s32[]{:S(2)}) async-start(), calls=%async_computation.18 | async-start | bytes 5160960 | tf_op jit(solution)/shard_map/psum | solution.py:339
  759.3 2.0 copy-start.7
  761.4 5.9 copy-start.11
  960.9 340.0 %copy-start.12 = (f32[256,3360]{0,1:T(8,128)S(1)}, f32[256,3360]{0,1:T(8,128)}, u32[]{:S(2)}) copy-start(f32[256,3360]{0,1:T(8,128)} %convert_element_type.222) | copy-start | bytes 10321924
  1416.5 5.5 copy-start.35
  1477.9 3.1 copy-start.31
  1477.9 4.7 copy-start.1
  (13 other events, 13.5 us)
Sparse Core Ops, SparseCore 0:
  9.6 57.3 all-gather.4
  68.5 34.8 all-gather.6
  105.6 148.7 all-gather.8
  256.4 146.6 all-gather.10
  436.4 33.1 reduce-scatter.15
  507.9 67.5 reduce-scatter.13
  579.4 378.5 reduce-scatter.9
  961.9 335.9 reduce-scatter.11
  1302.8 113.6 all-reduce.22
  1419.5 58.4 all-reduce.24
